TPU v7x, 32 devices: a whole 2x2x4 slice. The times are simulated.
32 devices in a mesh: gx: 4 (over x, core), gy: 2 (over y), gz: 4 (over z).
Axes of the slice: x: 2, y: 2, z: 4, core: 2. Of those that a mesh axis runs over, the one named last changes fastest.
Arguments:
- right_side: float32 [32, 32, 512], P('gx', 'gy', 'gz'), may hold values from -6 to 6
- conductance: float32 [32, 32, 512], P('gx', 'gy', 'gz'), may hold values from 0.25 to 4
- extents: int32 [4, 2, 4], P('gx', 'gy', 'gz'), may hold values from 64 to 128, as said below
- coarse_factor: bfloat16 [32, 32], replicated, may hold values from -1 to 3, as said below
Outputs:
- solution_field: float32 [32, 32, 512], P('gx', 'gy', 'gz')
- residual: float32 [32, 32, 512], P('gx', 'gy', 'gz')
Inputs may be any that keep to these rules, and one draw needn't show every extreme that they name: `extents`: cells of a block whose third local index is below its count are fluid, the others padding; in every draw some block has all 128 layers fluid. `coarse_factor`: lower triangular with a positive diagonal.
All inputs are finite; a program needn't handle non-finite values.
Results may differ from a plain program's by a relative error of at most 0.0003.
Values sent between devices are 32-bit elements; how exact they have to be, the bound alone decides.
A program may use at most 64 MiB of HBM per device.

v0:
```python
import jax
import jax.numpy as jnp
from jax import lax
from jax.sharding import PartitionSpec as P

ITERS = 2


OMEGA = 0.8


def extended(block, sides, width):
    for axis, dim in sides:
        count = lax.axis_size(axis)
        forward = [(i, i + 1) for i in range(count - 1)]
        backward = [(target, source) for source, target in forward]
        low = lax.ppermute(
            lax.slice_in_dim(block, block.shape[dim] - width, None, axis=dim), axis, forward
        )
        high = lax.ppermute(lax.slice_in_dim(block, 0, width, axis=dim), axis, backward)
        block = jnp.concatenate([low, block, high], axis=dim)
    return block


def neighbour_slices():
    inner = slice(1, -1)
    return [
        (slice(2, None), inner, inner),
        (slice(None, -2), inner, inner),
        (inner, slice(2, None), inner),
        (inner, slice(None, -2), inner),
        (inner, inner, slice(2, None)),
        (inner, inner, slice(None, -2)),
    ]


def face_terms(padded, cond_padded):
    centre = (slice(1, -1), slice(1, -1), slice(1, -1))
    value_mid = padded[centre]
    cond_mid = cond_padded[centre]
    summed = jnp.zeros_like(value_mid)
    for place in neighbour_slices():
        summed = summed + 0.5 * (cond_mid + cond_padded[place]) * (value_mid - padded[place])
    return summed


def coef_total(cond_padded):
    centre = (slice(1, -1), slice(1, -1), slice(1, -1))
    cond_mid = cond_padded[centre]
    summed = jnp.zeros_like(cond_mid)
    for place in neighbour_slices():
        summed = summed + 0.5 * (cond_mid + cond_padded[place])
    return summed


def interior(field):
    return field[1:-1, 1:-1, 1:-1]


def pool_sum(field):
    first, second, third = field.shape
    return field.reshape(first // 2, 2, second // 2, 2, third // 2, 2).sum(axis=(1, 3, 5))


def pool_max(field):
    first, second, third = field.shape
    return field.reshape(first // 2, 2, second // 2, 2, third // 2, 2).max(axis=(1, 3, 5))


def expand(field):
    first, second, third = field.shape
    wide = jnp.broadcast_to(field[:, None, :, None, :, None], (first, 2, second, 2, third, 2))
    return wide.reshape(2 * first, 2 * second, 2 * third)


def make_level(cond_padded, fluid, scale):
    inverse = fluid / (scale * coef_total(cond_padded) + 1.0 - fluid)
    return (cond_padded, fluid, scale, inverse)


def apply_level(field, level):
    padded = extended(field, (("gx", 0), ("gy", 1), ("gz", 2)), 1)
    return level[2] * level[1] * face_terms(padded, level[0])


def cycle(resid, levels):
    fine = levels[0]
    coarse_level = levels[1]
    first = OMEGA * fine[3] * resid
    image = apply_level(first, fine)
    below = OMEGA * coarse_level[3] * pool_sum(resid - image)
    return first + fine[1] * expand(below)


def selector(length):
    place = jnp.arange(length + 2)
    which = jnp.where(place == 0, 0, jnp.where(place == length + 1, 2, 1))
    return (which[:, None] == jnp.arange(3)[None, :]).astype(jnp.float32)


def on_device(right_side, conductance, extents, coarse_factor):
    factor = coarse_factor.astype(jnp.float32)
    size_x, size_y, size_z = right_side.shape
    block_cells = size_x * size_y * size_z
    layer = lax.broadcasted_iota(jnp.int32, right_side.shape, 2)
    fluid = (layer < extents[0, 0, 0]).astype(jnp.float32)
    fluid_mid = pool_max(fluid)
    cond_mid = pool_sum(conductance) / 8.0
    cond_padded = extended(cond_mid, (("gx", 0), ("gy", 1), ("gz", 2)), 1)
    coarse_level = make_level(cond_padded, fluid_mid, 4.0)
    stacked = extended(jnp.stack([conductance, fluid]), (("gx", 1), ("gy", 2), ("gz", 3)), 2)
    cond_wide = stacked[0]
    fluid_wide = interior(stacked[1])
    inverse_wide = fluid_wide / (coef_total(cond_wide) + 1.0 - fluid_wide)
    fine_level = (interior(cond_wide), fluid, 1.0, interior(inverse_wide))
    levels = [fine_level, coarse_level]
    index_x = lax.axis_index("gx")
    index_y = lax.axis_index("gy")
    index_z = lax.axis_index("gz")
    count_x = lax.axis_size("gx")
    count_y = lax.axis_size("gy")
    count_z = lax.axis_size("gz")
    offsets = jnp.arange(3, dtype=jnp.int32) - 1
    near_x = jnp.clip(index_x + offsets, 0, count_x - 1)
    near_y = jnp.clip(index_y + offsets, 0, count_y - 1)
    near_z = jnp.clip(index_z + offsets, 0, count_z - 1)
    near_flat = (near_x[:, None, None] * count_y + near_y[None, :, None]) * count_z + near_z[
        None, None, :
    ]
    select_x = selector(size_x)
    select_y = selector(size_y)
    select_z = selector(size_z)

    def precondition(resid):
        second = cycle(resid, levels)
        smoothed_wide = None
        pair = extended(jnp.stack([second, resid]), (("gx", 1), ("gy", 2), ("gz", 3)), 2)
        image_wide = fluid_wide * face_terms(pair[0], cond_wide)
        smoothed_wide = interior(pair[0]) + OMEGA * inverse_wide * (interior(pair[1]) - image_wide)
        smoothed = interior(smoothed_wide)
        block_mean = jnp.sum(resid) / block_cells
        local_product = jnp.sum(resid * smoothed)
        means = lax.all_gather(block_mean.reshape(1), ("gx", "gy", "gz"), axis=0, tiled=True)
        product = lax.psum(local_product, ("gx", "gy", "gz"))
        coarse = jax.scipy.linalg.cho_solve((factor, True), means)
        table = coarse[near_flat]
        precond = smoothed + fluid * table[1, 1, 1]
        inner_value = product + block_cells * jnp.sum(means * coarse)
        precond_wide = None
        coarse_wide = jnp.einsum(
            "abc,ia,jb,kc->ijk",
            table,
            select_x,
            select_y,
            select_z,
            precision=lax.Precision.HIGHEST,
        )
        precond_wide = smoothed_wide + fluid_wide * coarse_wide
        return (precond_wide, precond, inner_value)

    resid = fluid * right_side
    solution = jnp.zeros_like(resid)
    precond_wide, precond, inner_now = precondition(resid)
    direction = precond
    direction_wide = precond_wide
    for step in range(ITERS):
        padded = direction_wide
        image = fluid * face_terms(padded, fine_level[0])
        alpha = inner_now / lax.psum(jnp.sum(direction * image), ("gx", "gy", "gz"))
        solution = solution + alpha * direction
        resid = resid - alpha * image
        if step + 1 < ITERS:
            precond_wide, precond, inner_next = precondition(resid)
            ratio = inner_next / inner_now
            direction = precond + ratio * direction
            direction_wide = precond_wide + ratio * direction_wide
            inner_now = inner_next
    return (solution, resid)


def solution(mesh):
    in_specs = (P("gx", "gy", "gz"), P("gx", "gy", "gz"), P("gx", "gy", "gz"), P())
    out_specs = (P("gx", "gy", "gz"), P("gx", "gy", "gz"))
    return jax.shard_map(
        on_device, mesh=mesh, in_specs=in_specs, out_specs=out_specs, check_vma=False
    )
```

profile of v0, /device:TPU:0, one launch (start us, length us, event | category | flops | bytes accessed | tf_op | source)
XLA Modules:
  0.0 364.0 jit_solution(15990897442680924383)
XLA Ops:
  6.5 6.3 %reshape.132 = f32[4,2,8,2,64,2]{5,4,3,2,1,0:T(8,128)} reshape(f32[8,16,128]{2,1,0:T(8,128)} %param.7) | data formatting | bytes 131072 | tf_op jit(solution)/shard_map/reshape | solution.py:62
  16.7 5.1 %collective-permute-start.7 = (f32[1,8,64]{2,1,0:T(8,128)S(1)}, f32[1,8,64]{2,1,0:T(8,128)S(1)}, u32[]{:S(2)}, u32[]{:S(2)}) collective-permute-start(f32[1,8,64]{2,1,0:T(8,128)S(1)} %get-tuple-element.68), channel_id=1, source_target_pairs={{0,8},{8,16},{16,24},{1,9},{9,17},{17,25},{2,10},{10,18},{18,26},{... | collective-permute-start | bytes 6152 | tf_op jit(solution)/shard_map/ppermute | solution.py:17
  26.0 4.5 %collective-permute-start.2 = (f32[2,12,2,128]{3,2,1,0:T(2,128)S(1)}, f32[2,12,2,128]{3,2,1,0:T(2,128)S(1)}, u32[]{:S(2)}, u32[]{:S(2)}) collective-permute-start(f32[2,12,2,128]{3,2,1,0:T(2,128)S(1)} %get-tuple-element.41), channel_id=1, source_target_pairs={{0,4},{1,5},{2,6},{3,7},{8,12},{9,13},{10,14},{11,15},{16,20},{17,... | collective-permute-start | bytes 73736 | tf_op jit(solution)/shard_map/ppermute | solution.py:17
  31.9 4.5 %collective-permute-start.9 = (f32[6,1,64]{2,1,0:T(1,128)S(1)}, f32[6,1,64]{2,1,0:T(1,128)S(1)}, u32[]{:S(2)}, u32[]{:S(2)}) collective-permute-start(f32[6,1,64]{2,1,0:T(1,128)S(1)} %get-tuple-element.66), channel_id=1, source_target_pairs={{0,4},{1,5},{2,6},{3,7},{8,12},{9,13},{10,14},{11,15},{16,20},{17,... | collective-permute-start | bytes 4616 | tf_op jit(solution)/shard_map/ppermute | solution.py:17
  38.0 4.6 %collective-permute-start.4 = (f32[2,12,20,2]{3,2,1,0:T(8,128)S(1)}, f32[2,12,20,2]{3,2,1,0:T(8,128)S(1)}, u32[]{:S(2)}, u32[]{:S(2)}) collective-permute-start(f32[2,12,20,2]{3,2,1,0:T(8,128)S(1)} %get-tuple-element.35), channel_id=1, source_target_pairs={{0,1},{1,2},{2,3},{4,5},{5,6},{6,7},{8,9},{9,10},{10,11},{12,13},{... | collective-permute-start | bytes 11528 | tf_op jit(solution)/shard_map/ppermute | solution.py:17
  42.6 5.5 %collective-permute-done.5 = f32[2,12,20,2]{3,2,1,0:T(8,128)S(1)} collective-permute-done((f32[2,12,20,2]{3,2,1,0:T(8,128)S(1)}, f32[2,12,20,2]{3,2,1,0:T(8,128)S(1)}, u32[]{:S(2)}, u32[]{:S(2)}) %collective-permute-start.5) | collective-permute-done | bytes 3872 | tf_op jit(solution)/shard_map/ppermute | solution.py:20
  55.3 4.4 %collective-permute-start.11 = (f32[6,10,1]{2,1,0:T(8,128)S(1)}, f32[6,10,1]{2,1,0:T(8,128)S(1)}, u32[]{:S(2)}, u32[]{:S(2)}) collective-permute-start(f32[6,10,1]{2,1,0:T(8,128)S(1)} %get-tuple-element.65), channel_id=1, source_target_pairs={{0,1},{1,2},{2,3},{4,5},{5,6},{6,7},{8,9},{9,10},{10,11},{12,13},{... | collective-permute-start | bytes 728 | tf_op jit(solution)/shard_map/ppermute | solution.py:17
  61.7 40.5 %all-reduce = f32[32]{0:T(128)S(1)} all-reduce(f32[32]{0:T(128)S(1)} %dynamic-update-slice), channel_id=1, replica_groups=mesh['gx'=4,'gy'=2,'gz'=4] {'gx','gy','gz'}, use_global_device_ids=true, to_apply=%add | all-reduce | flops 32 | bytes 256
  103.6 4.5 %collective-permute-start.15 = (f32[10,1,128]{2,1,0:T(1,128)S(1)}, f32[10,1,128]{2,1,0:T(1,128)S(1)}, u32[]{:S(2)}, u32[]{:S(2)}) collective-permute-start(f32[10,1,128]{2,1,0:T(1,128)S(1)} %get-tuple-element.55), channel_id=1, source_target_pairs={{0,4},{1,5},{2,6},{3,7},{8,12},{9,13},{10,14},{11,15},{16,20},{17,... | collective-permute-start | bytes 15368 | tf_op jit(solution)/shard_map/ppermute | solution.py:17
  120.2 5.5 %reshape.133 = f32[4,2,8,2,64,2]{5,4,3,2,1,0:T(8,128)} reshape(f32[8,16,128]{2,1,0:T(8,128)S(1)} %get-tuple-element.18) | data formatting | bytes 131072 | tf_op jit(solution)/shard_map/reshape | solution.py:62
  130.9 4.0 %reshape.134 = f32[8,16,128]{2,1,0:T(8,128)S(1)} reshape(f32[4,2,8,2,64,2]{5,4,3,2,1,0:T(8,128)} %broadcast_in_dim.35) | data formatting | bytes 131072 | tf_op jit(solution)/shard_map/reshape | solution.py:73
  141.5 4.5 %collective-permute-start.20 = (f32[2,12,2,128]{3,2,1,0:T(2,128)S(1)}, f32[2,12,2,128]{3,2,1,0:T(2,128)S(1)}, u32[]{:S(2)}, u32[]{:S(2)}) collective-permute-start(f32[2,12,2,128]{3,2,1,0:T(2,128)S(1)} %get-tuple-element.39), channel_id=1, source_target_pairs={{0,4},{1,5},{2,6},{3,7},{8,12},{9,13},{10,14},{11,15},{16,20},{17,... | collective-permute-start | bytes 73736 | tf_op jit(solution)/shard_map/ppermute | solution.py:17
  149.0 4.6 %collective-permute-start.22 = (f32[2,12,20,2]{3,2,1,0:T(8,128)S(1)}, f32[2,12,20,2]{3,2,1,0:T(8,128)S(1)}, u32[]{:S(2)}, u32[]{:S(2)}) collective-permute-start(f32[2,12,20,2]{3,2,1,0:T(8,128)S(1)} %get-tuple-element.33), channel_id=1, source_target_pairs={{0,1},{1,2},{2,3},{4,5},{5,6},{6,7},{8,9},{9,10},{10,11},{12,13},{... | collective-permute-start | bytes 11528 | tf_op jit(solution)/shard_map/ppermute | solution.py:17
  155.0 4.5 %collective-permute-done.23 = f32[2,12,20,2]{3,2,1,0:T(8,128)S(1)} collective-permute-done((f32[2,12,20,2]{3,2,1,0:T(8,128)S(1)}, f32[2,12,20,2]{3,2,1,0:T(8,128)S(1)}, u32[]{:S(2)}, u32[]{:S(2)}) %collective-permute-start.23) | collective-permute-done | bytes 3872 | tf_op jit(solution)/shard_map/ppermute | solution.py:20
  163.3 42.3 %all-reduce.3 = (f32[]{:T(128)}, f32[]{:T(128)}) all-reduce(f32[]{:T(128)} %get-tuple-element.4, f32[]{:T(128)} %get-tuple-element.3), channel_id=1, replica_groups=mesh['gx'=4,'gy'=2,'gz'=4] {'gx','gy','gz'}, use_global_device_ids=true, to_apply=%region_4.5 | all-reduce | flops 2 | bytes 16 | tf_op jit(solution)/shard_map/psum | solution.py:144
  213.4 4.5 %collective-permute-start.27 = (f32[10,1,128]{2,1,0:T(1,128)S(1)}, f32[10,1,128]{2,1,0:T(1,128)S(1)}, u32[]{:S(2)}, u32[]{:S(2)}) collective-permute-start(f32[10,1,128]{2,1,0:T(1,128)S(1)} %get-tuple-element.53), channel_id=1, source_target_pairs={{0,4},{1,5},{2,6},{3,7},{8,12},{9,13},{10,14},{11,15},{16,20},{17,... | collective-permute-start | bytes 15368 | tf_op jit(solution)/shard_map/ppermute | solution.py:17
  225.2 4.1 %collective-permute-done.28 = f32[10,18,1]{2,1,0:T(8,128)S(1)} collective-permute-done((f32[10,18,1]{2,1,0:T(8,128)S(1)}, f32[10,18,1]{2,1,0:T(8,128)S(1)}, u32[]{:S(2)}, u32[]{:S(2)}) %collective-permute-start.28) | collective-permute-done | bytes 752 | tf_op jit(solution)/shard_map/ppermute | solution.py:20
  229.4 5.5 %reshape.136 = f32[4,2,8,2,64,2]{5,4,3,2,1,0:T(8,128)} reshape(f32[8,16,128]{2,1,0:T(8,128)S(1)} %fusion.55) | data formatting | bytes 131072 | tf_op jit(solution)/shard_map/reshape | solution.py:62
  240.0 4.0 %reshape.137 = f32[8,16,128]{2,1,0:T(8,128)S(1)} reshape(f32[4,2,8,2,64,2]{5,4,3,2,1,0:T(8,128)} %broadcast_in_dim.61) | data formatting | bytes 131072 | tf_op jit(solution)/shard_map/reshape | solution.py:73
  250.6 4.5 %collective-permute-start.32 = (f32[2,12,2,128]{3,2,1,0:T(2,128)S(1)}, f32[2,12,2,128]{3,2,1,0:T(2,128)S(1)}, u32[]{:S(2)}, u32[]{:S(2)}) collective-permute-start(f32[2,12,2,128]{3,2,1,0:T(2,128)S(1)} %get-tuple-element.37), channel_id=1, source_target_pairs={{0,4},{1,5},{2,6},{3,7},{8,12},{9,13},{10,14},{11,15},{16,20},{17,... | collective-permute-start | bytes 73736 | tf_op jit(solution)/shard_map/ppermute | solution.py:17
  258.1 4.6 %collective-permute-start.34 = (f32[2,12,20,2]{3,2,1,0:T(8,128)S(1)}, f32[2,12,20,2]{3,2,1,0:T(8,128)S(1)}, u32[]{:S(2)}, u32[]{:S(2)}) collective-permute-start(f32[2,12,20,2]{3,2,1,0:T(8,128)S(1)} %get-tuple-element.31), channel_id=1, source_target_pairs={{0,1},{1,2},{2,3},{4,5},{5,6},{6,7},{8,9},{9,10},{10,11},{12,13},{... | collective-permute-start | bytes 11528 | tf_op jit(solution)/shard_map/ppermute | solution.py:17
  262.7 5.0 %collective-permute-done.35 = f32[2,12,20,2]{3,2,1,0:T(8,128)S(1)} collective-permute-done((f32[2,12,20,2]{3,2,1,0:T(8,128)S(1)}, f32[2,12,20,2]{3,2,1,0:T(8,128)S(1)}, u32[]{:S(2)}, u32[]{:S(2)}) %collective-permute-start.35) | collective-permute-done | bytes 3872 | tf_op jit(solution)/shard_map/ppermute | solution.py:20
  272.4 43.4 %all-reduce.2 = (f32[]{:T(128)}, f32[32]{0:T(128)S(1)}) all-reduce(f32[]{:T(128)} %get-tuple-element.6, f32[32]{0:T(128)S(1)} %dynamic-update-slice.1), channel_id=1, replica_groups=mesh['gx'=4,'gy'=2,'gz'=4] {'gx','gy','gz'}, use_global_device_ids=true, to_apply=%region_11.13 | all-reduce | flops 33 | bytes 264 | tf_op jit(solution)/shard_map/psum | solution.py:144
  321.8 40.1 %psum.31 = f32[]{:T(128)} all-reduce(f32[]{:T(128)} %get-tuple-element.11), channel_id=1, replica_groups=mesh['gx'=4,'gy'=2,'gz'=4] {'gx','gy','gz'}, use_global_device_ids=true, to_apply=%region_15.17 | all-reduce | flops 1 | bytes 8 | tf_op jit(solution)/shard_map/psum | solution.py:169
  (154 shorter events, 95.4 us)
Async XLA Ops:
  2.0 22.6 %collective-permute-start.1 = (f32[2,2,16,128]{3,2,1,0:T(8,128)S(1)}, f32[2,2,16,128]{3,2,1,0:T(8,128)S(1)}, u32[]{:S(2)}, u32[]{:S(2)}) collective-permute-start(f32[2,2,16,128]{3,2,1,0:T(8,128)S(1)} %get-tuple-element.48), channel_id=1, source_target_pairs={{8,0},{16,8},{24,16},{9,1},{17,9},{25,17},{10,2},{18,10},{26,18},{... | collective-permute-start | bytes 98312 | tf_op jit(solution)/shard_map/ppermute | solution.py:20
  3.4 21.3 %collective-permute-start = (f32[2,2,16,128]{3,2,1,0:T(8,128)S(1)}, f32[2,2,16,128]{3,2,1,0:T(8,128)S(1)}, u32[]{:S(2)}, u32[]{:S(2)}) collective-permute-start(f32[2,2,16,128]{3,2,1,0:T(8,128)S(1)} %get-tuple-element.47), channel_id=1, source_target_pairs={{0,8},{8,16},{16,24},{1,9},{9,17},{17,25},{2,10},{10,18},{18,26},{... | collective-permute-start | bytes 98312 | tf_op jit(solution)/shard_map/ppermute | solution.py:17
  15.4 15.2 %collective-permute-start.6 = (f32[1,8,64]{2,1,0:T(8,128)S(1)}, f32[1,8,64]{2,1,0:T(8,128)S(1)}, u32[]{:S(2)}, u32[]{:S(2)}) collective-permute-start(f32[1,8,64]{2,1,0:T(8,128)S(1)} %get-tuple-element.69), channel_id=1, source_target_pairs={{8,0},{16,8},{24,16},{9,1},{17,9},{25,17},{10,2},{18,10},{26,18},{... | collective-permute-start | bytes 6152 | tf_op jit(solution)/shard_map/ppermute | solution.py:20
  16.7 13.9 %collective-permute-start.7 = (f32[1,8,64]{2,1,0:T(8,128)S(1)}, f32[1,8,64]{2,1,0:T(8,128)S(1)}, u32[]{:S(2)}, u32[]{:S(2)}) collective-permute-start(f32[1,8,64]{2,1,0:T(8,128)S(1)} %get-tuple-element.68), channel_id=1, source_target_pairs={{0,8},{8,16},{16,24},{1,9},{9,17},{17,25},{2,10},{10,18},{18,26},{... | collective-permute-start | bytes 6152 | tf_op jit(solution)/shard_map/ppermute | solution.py:17
  24.7 11.7 %collective-permute-start.3 = (f32[2,12,2,128]{3,2,1,0:T(2,128)S(1)}, f32[2,12,2,128]{3,2,1,0:T(2,128)S(1)}, u32[]{:S(2)}, u32[]{:S(2)}) collective-permute-start(f32[2,12,2,128]{3,2,1,0:T(2,128)S(1)} %get-tuple-element.42), channel_id=1, source_target_pairs={{4,0},{5,1},{6,2},{7,3},{12,8},{13,9},{14,10},{15,11},{20,16},{21,... | collective-permute-start | bytes 73736 | tf_op jit(solution)/shard_map/ppermute | solution.py:20
  26.0 10.5 %collective-permute-start.2 = (f32[2,12,2,128]{3,2,1,0:T(2,128)S(1)}, f32[2,12,2,128]{3,2,1,0:T(2,128)S(1)}, u32[]{:S(2)}, u32[]{:S(2)}) collective-permute-start(f32[2,12,2,128]{3,2,1,0:T(2,128)S(1)} %get-tuple-element.41), channel_id=1, source_target_pairs={{0,4},{1,5},{2,6},{3,7},{8,12},{9,13},{10,14},{11,15},{16,20},{17,... | collective-permute-start | bytes 73736 | tf_op jit(solution)/shard_map/ppermute | solution.py:17
  30.6 11.9 %collective-permute-start.8 = (f32[6,1,64]{2,1,0:T(1,128)S(1)}, f32[6,1,64]{2,1,0:T(1,128)S(1)}, u32[]{:S(2)}, u32[]{:S(2)}) collective-permute-start(f32[6,1,64]{2,1,0:T(1,128)S(1)} %get-tuple-element.67), channel_id=1, source_target_pairs={{4,0},{5,1},{6,2},{7,3},{12,8},{13,9},{14,10},{15,11},{20,16},{21,... | collective-permute-start | bytes 4616 | tf_op jit(solution)/shard_map/ppermute | solution.py:20
  31.9 10.7 %collective-permute-start.9 = (f32[6,1,64]{2,1,0:T(1,128)S(1)}, f32[6,1,64]{2,1,0:T(1,128)S(1)}, u32[]{:S(2)}, u32[]{:S(2)}) collective-permute-start(f32[6,1,64]{2,1,0:T(1,128)S(1)} %get-tuple-element.66), channel_id=1, source_target_pairs={{0,4},{1,5},{2,6},{3,7},{8,12},{9,13},{10,14},{11,15},{16,20},{17,... | collective-permute-start | bytes 4616 | tf_op jit(solution)/shard_map/ppermute | solution.py:17
  36.7 11.4 %collective-permute-start.5 = (f32[2,12,20,2]{3,2,1,0:T(8,128)S(1)}, f32[2,12,20,2]{3,2,1,0:T(8,128)S(1)}, u32[]{:S(2)}, u32[]{:S(2)}) collective-permute-start(f32[2,12,20,2]{3,2,1,0:T(8,128)S(1)} %get-tuple-element.36), channel_id=1, source_target_pairs={{1,0},{2,1},{3,2},{5,4},{6,5},{7,6},{9,8},{10,9},{11,10},{13,12},{... | collective-permute-start | bytes 11528 | tf_op jit(solution)/shard_map/ppermute | solution.py:20
  38.0 11.3 %collective-permute-start.4 = (f32[2,12,20,2]{3,2,1,0:T(8,128)S(1)}, f32[2,12,20,2]{3,2,1,0:T(8,128)S(1)}, u32[]{:S(2)}, u32[]{:S(2)}) collective-permute-start(f32[2,12,20,2]{3,2,1,0:T(8,128)S(1)} %get-tuple-element.35), channel_id=1, source_target_pairs={{0,1},{1,2},{2,3},{4,5},{5,6},{6,7},{8,9},{9,10},{10,11},{12,13},{... | collective-permute-start | bytes 11528 | tf_op jit(solution)/shard_map/ppermute | solution.py:17
  50.9 51.4 %collective-permute-start.12 = (f32[1,16,128]{2,1,0:T(8,128)S(1)}, f32[1,16,128]{2,1,0:T(8,128)S(1)}, u32[]{:S(2)}, u32[]{:S(2)}) collective-permute-start(f32[1,16,128]{2,1,0:T(8,128)S(1)} %get-tuple-element.63), channel_id=1, source_target_pairs={{8,0},{16,8},{24,16},{9,1},{17,9},{25,17},{10,2},{18,10},{26,18},{... | collective-permute-start | bytes 24584 | tf_op jit(solution)/shard_map/ppermute | solution.py:20
  52.2 50.1 %collective-permute-start.13 = (f32[1,16,128]{2,1,0:T(8,128)S(1)}, f32[1,16,128]{2,1,0:T(8,128)S(1)}, u32[]{:S(2)}, u32[]{:S(2)}) collective-permute-start(f32[1,16,128]{2,1,0:T(8,128)S(1)} %get-tuple-element.62), channel_id=1, source_target_pairs={{0,8},{8,16},{16,24},{1,9},{9,17},{17,25},{2,10},{10,18},{18,26},{... | collective-permute-start | bytes 24584 | tf_op jit(solution)/shard_map/ppermute | solution.py:17
  55.3 73.0 %collective-permute-start.11 = (f32[6,10,1]{2,1,0:T(8,128)S(1)}, f32[6,10,1]{2,1,0:T(8,128)S(1)}, u32[]{:S(2)}, u32[]{:S(2)}) collective-permute-start(f32[6,10,1]{2,1,0:T(8,128)S(1)} %get-tuple-element.65), channel_id=1, source_target_pairs={{0,1},{1,2},{2,3},{4,5},{5,6},{6,7},{8,9},{9,10},{10,11},{12,13},{... | collective-permute-start | bytes 728 | tf_op jit(solution)/shard_map/ppermute | solution.py:17
  60.4 67.8 %collective-permute-start.10 = (f32[6,10,1]{2,1,0:T(8,128)S(1)}, f32[6,10,1]{2,1,0:T(8,128)S(1)}, u32[]{:S(2)}, u32[]{:S(2)}) collective-permute-start(f32[6,10,1]{2,1,0:T(8,128)S(1)} %get-tuple-element.64), channel_id=1, source_target_pairs={{1,0},{2,1},{3,2},{5,4},{6,5},{7,6},{9,8},{10,9},{11,10},{13,12},{... | collective-permute-start | bytes 728 | tf_op jit(solution)/shard_map/ppermute | solution.py:20
  109.6 6.5 %collective-permute-start.17 = (f32[10,18,1]{2,1,0:T(8,128)S(1)}, f32[10,18,1]{2,1,0:T(8,128)S(1)}, u32[]{:S(2)}, u32[]{:S(2)}) collective-permute-start(f32[10,18,1]{2,1,0:T(8,128)S(1)} %get-tuple-element.52), channel_id=1, source_target_pairs={{0,1},{1,2},{2,3},{4,5},{5,6},{6,7},{8,9},{9,10},{10,11},{12,13},{... | collective-permute-start | bytes 2168 | tf_op jit(solution)/shard_map/ppermute | solution.py:17
  113.2 6.8 %collective-permute-start.16 = (f32[10,18,1]{2,1,0:T(8,128)S(1)}, f32[10,18,1]{2,1,0:T(8,128)S(1)}, u32[]{:S(2)}, u32[]{:S(2)}) collective-permute-start(f32[10,18,1]{2,1,0:T(8,128)S(1)} %get-tuple-element.51), channel_id=1, source_target_pairs={{1,0},{2,1},{3,2},{5,4},{6,5},{7,6},{9,8},{10,9},{11,10},{13,12},{... | collective-permute-start | bytes 2168 | tf_op jit(solution)/shard_map/ppermute | solution.py:20
  140.2 6.7 %collective-permute-start.21 = (f32[2,12,2,128]{3,2,1,0:T(2,128)S(1)}, f32[2,12,2,128]{3,2,1,0:T(2,128)S(1)}, u32[]{:S(2)}, u32[]{:S(2)}) collective-permute-start(f32[2,12,2,128]{3,2,1,0:T(2,128)S(1)} %get-tuple-element.40), channel_id=1, source_target_pairs={{4,0},{5,1},{6,2},{7,3},{12,8},{13,9},{14,10},{15,11},{20,16},{21,... | collective-permute-start | bytes 73736 | tf_op jit(solution)/shard_map/ppermute | solution.py:20
  141.5 6.1 %collective-permute-start.20 = (f32[2,12,2,128]{3,2,1,0:T(2,128)S(1)}, f32[2,12,2,128]{3,2,1,0:T(2,128)S(1)}, u32[]{:S(2)}, u32[]{:S(2)}) collective-permute-start(f32[2,12,2,128]{3,2,1,0:T(2,128)S(1)} %get-tuple-element.39), channel_id=1, source_target_pairs={{0,4},{1,5},{2,6},{3,7},{8,12},{9,13},{10,14},{11,15},{16,20},{17,... | collective-permute-start | bytes 73736 | tf_op jit(solution)/shard_map/ppermute | solution.py:17
  147.7 11.7 %collective-permute-start.23 = (f32[2,12,20,2]{3,2,1,0:T(8,128)S(1)}, f32[2,12,20,2]{3,2,1,0:T(8,128)S(1)}, u32[]{:S(2)}, u32[]{:S(2)}) collective-permute-start(f32[2,12,20,2]{3,2,1,0:T(8,128)S(1)} %get-tuple-element.34), channel_id=1, source_target_pairs={{1,0},{2,1},{3,2},{5,4},{6,5},{7,6},{9,8},{10,9},{11,10},{13,12},{... | collective-permute-start | bytes 11528 | tf_op jit(solution)/shard_map/ppermute | solution.py:20
  149.0 11.6 %collective-permute-start.22 = (f32[2,12,20,2]{3,2,1,0:T(8,128)S(1)}, f32[2,12,20,2]{3,2,1,0:T(8,128)S(1)}, u32[]{:S(2)}, u32[]{:S(2)}) collective-permute-start(f32[2,12,20,2]{3,2,1,0:T(8,128)S(1)} %get-tuple-element.33), channel_id=1, source_target_pairs={{0,1},{1,2},{2,3},{4,5},{5,6},{6,7},{8,9},{9,10},{10,11},{12,13},{... | collective-permute-start | bytes 11528 | tf_op jit(solution)/shard_map/ppermute | solution.py:17
  221.7 7.6 %collective-permute-start.28 = (f32[10,18,1]{2,1,0:T(8,128)S(1)}, f32[10,18,1]{2,1,0:T(8,128)S(1)}, u32[]{:S(2)}, u32[]{:S(2)}) collective-permute-start(f32[10,18,1]{2,1,0:T(8,128)S(1)} %get-tuple-element.49), channel_id=1, source_target_pairs={{1,0},{2,1},{3,2},{5,4},{6,5},{7,6},{9,8},{10,9},{11,10},{13,12},{... | collective-permute-start | bytes 2168 | tf_op jit(solution)/shard_map/ppermute | solution.py:20
  250.6 6.1 %collective-permute-start.32 = (f32[2,12,2,128]{3,2,1,0:T(2,128)S(1)}, f32[2,12,2,128]{3,2,1,0:T(2,128)S(1)}, u32[]{:S(2)}, u32[]{:S(2)}) collective-permute-start(f32[2,12,2,128]{3,2,1,0:T(2,128)S(1)} %get-tuple-element.37), channel_id=1, source_target_pairs={{0,4},{1,5},{2,6},{3,7},{8,12},{9,13},{10,14},{11,15},{16,20},{17,... | collective-permute-start | bytes 73736 | tf_op jit(solution)/shard_map/ppermute | solution.py:17
  256.8 10.9 %collective-permute-start.35 = (f32[2,12,20,2]{3,2,1,0:T(8,128)S(1)}, f32[2,12,20,2]{3,2,1,0:T(8,128)S(1)}, u32[]{:S(2)}, u32[]{:S(2)}) collective-permute-start(f32[2,12,20,2]{3,2,1,0:T(8,128)S(1)} %get-tuple-element.32), channel_id=1, source_target_pairs={{1,0},{2,1},{3,2},{5,4},{6,5},{7,6},{9,8},{10,9},{11,10},{13,12},{... | collective-permute-start | bytes 11528 | tf_op jit(solution)/shard_map/ppermute | solution.py:20
  258.1 11.3 %collective-permute-start.34 = (f32[2,12,20,2]{3,2,1,0:T(8,128)S(1)}, f32[2,12,20,2]{3,2,1,0:T(8,128)S(1)}, u32[]{:S(2)}, u32[]{:S(2)}) collective-permute-start(f32[2,12,20,2]{3,2,1,0:T(8,128)S(1)} %get-tuple-element.31), channel_id=1, source_target_pairs={{0,1},{1,2},{2,3},{4,5},{5,6},{6,7},{8,9},{9,10},{10,11},{12,13},{... | collective-permute-start | bytes 11528 | tf_op jit(solution)/shard_map/ppermute | solution.py:17
  (15 other events, 134.7 us)
where the time goes:
time: 366 us; the launch traced here: 364 us
  blocking collectives  166 us (45%)
  starting transfers between devices  94.8 us (26%)
  waiting for transfers between devices  36.2 us (10%)
  local copies, waits for them, and re-layouts  34.6 us (9%)
  other arithmetic  21.4 us (6%)
  between operations  7.46 us (2%)
    psum x2, blocking collectives, precondition(): product = lax.psum(local_product, ('gx', 'gy', 'gz'))  85.6 us
    ppermute x18, starting transfers between devices, extended(): lax.ppermute(lax.slice_in_dim(block, block.shape[dim] - width, None, axis...  71.6 us
    unnamed x1, blocking collectives  40.5 us
    psum x1, blocking collectives, on_device(): alpha = inner_now / lax.psum(jnp.sum(direction * image), ('gx', 'gy', 'gz'))  40.1 us
    ppermute x18, starting transfers between devices, extended(): lax.ppermute(lax.slice_in_dim(block, 0, width, axis=dim), axis, backward)  23.2 us
    ppermute x18, waiting for transfers between devices, extended(): lax.ppermute(lax.slice_in_dim(block, 0, width, axis=dim), axis, backward)  23 us
    reshape x3, local copies, waits for them, and re-layouts, pool_sum(): field.reshape(first // 2, 2, second // 2, 2, third // 2, 2)  17.3 us
    ppermute x18, waiting for transfers between devices, extended(): lax.ppermute(lax.slice_in_dim(block, block.shape[dim] - width, None, axis...  13.2 us
  transfers between devices with their start and end apart: 36, of which 16 were waited for; matrix products, arithmetic and copies ran while one was open for 7% of the time, Pallas kernels for 0%

commit v1 on v0

v1 whole, which is shorter than its diff:
```python
import functools

import jax
import jax.numpy as jnp
from jax import lax
from jax.experimental import pallas as pl
from jax.experimental.pallas import tpu as pltpu
from jax.sharding import PartitionSpec as P

OMEGA = 0.8
HALO = 4
MESH = pl.DeviceIdType.MESH
HIGH = lax.Precision.HIGHEST
DIRS = [
    (dx, dy, dz)
    for dx in (-1, 0, 1)
    for dy in (-1, 0, 1)
    for dz in (-1, 0, 1)
    if (dx, dy, dz) != (0, 0, 0)
]


def code(dx, dy, dz):
    return (dx + 1) * 9 + (dy + 1) * 3 + dz + 1


def kernel(
    counts,
    rhs_ref,
    cond_ref,
    ext_ref,
    factor_ref,
    sol_ref,
    res_ref,
    h_out,
    p_out,
    e_out,
    x_in,
    h_in,
    p_in,
    e_in,
    av_out,
    h2_out,
    p2_out,
    x2_in,
    h2_in,
    p2_in,
    row_out,
    row2_out,
    gath,
    gath2,
    R,
    C,
    FL,
    FX,
    FY,
    FZ,
    INV,
    C1,
    IC,
    FIRST,
    SEC,
    V,
    U,
    YT,
    D0,
    AD0,
    AV1,
    send_a,
    recv_a,
    send_e,
    recv_e,
    send_b,
    recv_b,
    send_g,
    recv_g,
):
    ngx, ngy, ngz = counts
    n = ngx * ngy * ngz
    ix, iy, iz = lax.axis_index("gx"), lax.axis_index("gy"), lax.axis_index("gz")
    me = (ix * ngy + iy) * ngz + iz
    bx, by, bz = rhs_ref.shape
    ex, ey, ez = bx + 2 * HALO, by + 2 * HALO, 2 * bz
    group = 2 * HALO
    half = bz // 2
    f32 = jnp.float32

    def coords(flat):
        return (flat // (ngy * ngz), (flat // ngz) % ngy, flat % ngz)

    barrier = pltpu.get_barrier_semaphore()

    def greet(t, carry):
        pl.semaphore_signal(
            barrier, inc=1, device_id=coords((me + t) % n), device_id_type=MESH
        )
        return carry

    for buf in (x_in, h_in, p_in, e_in, x2_in, h2_in, p2_in):
        buf[...] = jnp.zeros(buf.shape, f32)
    lax.fori_loop(1, n, greet, 0)

    lane = lax.broadcasted_iota(jnp.int32, (ey, bz), 1)
    row8 = lax.broadcasted_iota(jnp.int32, (2 * HALO, bz), 0)

    def edge_tile(slab):
        return jnp.where(row8 < HALO, slab[: 2 * HALO], slab[by - 2 * HALO :])

    def pack(slabs):
        packed = jnp.zeros((ey, bz), f32)
        for at, (slab, tile) in enumerate(slabs):
            full = jnp.concatenate([slab, tile], axis=0)
            moved = pltpu.roll(full, (HALO + group * at) % bz, 1)
            packed = jnp.where(lane // group == at, moved, packed)
        return packed

    slabs = []
    for f, ref in enumerate((rhs_ref, cond_ref)):
        for x in range(bx):
            slab = ref[x]
            tile = edge_tile(slab)
            h_out[f, x] = tile
            slabs.append((slab, tile))
    p_out[...] = pack(slabs)
    own_limit = ext_ref[0, 0, 0]
    e_out[...] = jnp.full((1, bz), own_limit.astype(f32), f32)

    L = factor_ref[...].astype(f32)
    ri = lax.broadcasted_iota(jnp.int32, (n, n), 0)
    ci = lax.broadcasted_iota(jnp.int32, (n, n), 1)
    eye = ri == ci
    X = jnp.where(eye, 1.0 / jnp.where(eye, L, 1.0), 0.0)
    s = 1
    while s < n:
        pick = (ri // (2 * s) == ci // (2 * s)) & (ri % (2 * s) >= s) & (ci % (2 * s) < s)
        low = jnp.where(pick, L, 0.0)
        X = X - jnp.dot(
            X,
            jnp.dot(low, X, precision=HIGH, preferred_element_type=f32),
            precision=HIGH,
            preferred_element_type=f32,
        )
        s *= 2
    W = lax.dot_general(
        X, X, (((0,), (0,)), ((), ())), precision=HIGH, preferred_element_type=f32
    )

    pl.semaphore_wait(barrier, n - 1)

    def inside(d):
        dx, dy, dz = d
        ok = None
        for at, step, count in ((ix, dx, ngx), (iy, dy, ngy), (iz, dz, ngz)):
            if step == 0:
                continue
            here = (at + step >= 0) & (at + step < count)
            ok = here if ok is None else ok & here
        return ok

    def target(d):
        return (ix + d[0], iy + d[1], iz + d[2])

    def remote(src, dst, send, recv, d):
        return pltpu.make_async_remote_copy(
            src_ref=src,
            dst_ref=dst,
            send_sem=send,
            recv_sem=recv,
            device_id=target(d),
            device_id_type=MESH,
        )

    def x_part(dx):
        if dx == 0:
            return pl.ds(0, bx), pl.ds(HALO, bx)
        if dx == 1:
            return pl.ds(bx - HALO, HALO), pl.ds(0, HALO)
        return pl.ds(0, HALO), pl.ds(bx + HALO, HALO)

    def side(dx):
        return 0 if dx == 1 else 1

    def copies_a(d):
        dx, dy, dz = d
        k = code(*d)
        out = [remote(e_out, e_in.at[code(-dx, -dy, -dz)], send_e.at[k], recv_e.at[k], d)]
        if dz != 0:
            slot = code(-dx, -dy, -dz)
            out.append(remote(p_out, p_in.at[slot], send_a.at[k, 0], recv_a.at[k, 0], d))
        elif dy != 0:
            src, dst = x_part(dx)
            out.append(
                remote(
                    h_out.at[:, src],
                    h_in.at[side(dy), :, dst],
                    send_a.at[k, 0],
                    recv_a.at[k, 0],
                    d,
                )
            )
        else:
            src, _ = x_part(dx)
            for f, ref in enumerate((rhs_ref, cond_ref)):
                out.append(
                    remote(
                        ref.at[src],
                        x_in.at[side(dx), f],
                        send_a.at[k, f],
                        recv_a.at[k, f],
                        d,
                    )
                )
        return out

    def copies_b(d):
        dx, dy, dz = d
        k = code(*d)
        if dz != 0:
            slot = code(-dx, -dy, -dz)
            return [remote(p2_out, p2_in.at[slot], send_b.at[k], recv_b.at[k], d)]
        src, dst = x_part(dx)
        if dy != 0:
            return [
                remote(
                    h2_out.at[src], h2_in.at[side(dy), dst], send_b.at[k], recv_b.at[k], d
                )
            ]
        return [remote(av_out.at[src], x2_in.at[side(dx)], send_b.at[k], recv_b.at[k], d)]

    def start_all(copies):
        for d in DIRS:

            @pl.when(inside(d))
            def _():
                for c in copies(d):
                    c.start()

    def wait_all(copies):
        for d in DIRS:
            @pl.when(inside(tuple(-a for a in d)))
            def _():
                for c in copies(d):
                    c.wait_recv()

        for d in DIRS:

            @pl.when(inside(d))
            def _():
                for c in copies(d):
                    c.wait_send()

    start_all(copies_a)

    rowe = lax.broadcasted_iota(jnp.int32, (ey, bz), 0)
    low_lanes = (lane % group) < HALO

    def merge_h(h, *at):
        return jnp.where(row8 < HALO, h[(1,) + at], h[(0,) + at])

    def merge_p(p):
        merged = []
        for dx in (-1, 0, 1):

            def from_z(dy):
                return jnp.where(
                    low_lanes, p[code(dx, dy, 1)], p[code(dx, dy, -1)]
                ), jnp.where(low_lanes, p[code(dx, dy, -1)], p[code(dx, dy, 1)])

            mid = from_z(0)[1]
            up = from_z(1)[1]
            down = from_z(-1)[1]
            merged.append(
                jnp.where(rowe < by, mid, jnp.where(rowe < by + HALO, up, down))
            )
        return merged

    def where_from(x):
        if x < HALO:
            return 0, bx - HALO + x
        if x < HALO + bx:
            return 1, x - HALO
        return 2, x - HALO - bx

    def unpack(merged, x, f):
        which, slab = where_from(x)
        at = f * bx + slab
        return pltpu.roll(merged[which], (bz - HALO - group * at) % bz, 1)

    wait_all(copies_a)

    merged = merge_p(p_in)
    limits = []
    for dx in (-1, 0, 1):
        sides = []
        for dz in (0, 1, -1):

            def limit(dy):
                if (dx, dy, dz) == (0, 0, 0):
                    return e_out[...]
                return e_in[code(dx, dy, dz)]

            sides.append(
                jnp.where(rowe < by, limit(0), jnp.where(rowe < by + HALO, limit(1), limit(-1)))
            )
        limits.append((sides[0], jnp.where(lane < half, sides[1], sides[2])))
    flags, flags1 = [], []
    lane_f = lane.astype(f32)
    even_f = (lane - lane % 2).astype(f32)
    for a, b in limits:
        flags.append(
            jnp.concatenate([(lane_f < a).astype(f32), (lane_f < b).astype(f32)], axis=1)
        )
        flags1.append(
            jnp.concatenate([(even_f < a).astype(f32), (even_f < b).astype(f32)], axis=1)
        )
    for x in range(ex):
        which, _ = where_from(x)
        FL[x] = flags[which]
        for f, (ref, field) in enumerate(((rhs_ref, R), (cond_ref, C))):
            if which == 1:
                core = ref[x - HALO]
            elif which == 0:
                core = x_in[0, f, x]
            else:
                core = x_in[1, f, x - HALO - bx]
            a = jnp.concatenate([core, merge_h(h_in, f, x)], axis=0)
            whole = jnp.concatenate([a, unpack(merged, x, f)], axis=1)
            field[x] = whole * flags[which] if f == 0 else whole

    wide_lane = lax.broadcasted_iota(jnp.int32, (ey, ez), 1)
    wide_row = lax.broadcasted_iota(jnp.int32, (ey, ez), 0)
    odd_lane = wide_lane % 2 == 1
    odd_row = wide_row % 2 == 1

    def up_y(v, k=1):
        return pltpu.roll(v, k, 0)

    def dn_y(v, k=1):
        return pltpu.roll(v, ey - k, 0)

    def up_z(v, k=1):
        return pltpu.roll(v, k, 1)

    def dn_z(v, k=1):
        return pltpu.roll(v, ez - k, 1)

    def pool_yz(v):
        v = v + jnp.where(odd_row, up_y(v), dn_y(v))
        return v + jnp.where(odd_lane, up_z(v), dn_z(v))

    for x in range(ex):
        c = C[x]
        if x > 0:
            FX[x] = 0.5 * (C[x - 1] + c)
        FY[x] = 0.5 * (c + up_y(c))
        FZ[x] = 0.5 * (c + up_z(c))
    for x in range(1, ex - 1):
        fy, fz = FY[x], FZ[x]
        total = FX[x] + FX[x + 1] + fy + dn_y(fy) + fz + dn_z(fz)
        fl = FL[x]
        INV[x] = OMEGA * fl / (total + 1.0 - fl)
    for q in range(ex // 2):
        C1[q] = pool_yz(C[2 * q] + C[2 * q + 1]) * 0.125
    for q in range(1, ex // 2 - 1):
        c = C1[q]
        total = 3.0 * c + 0.5 * (
            C1[q - 1] + C1[q + 1] + up_y(c, 2) + dn_y(c, 2) + up_z(c, 2) + dn_z(c, 2)
        )
        fl = flags1[where_from(2 * q)[0]]
        IC[q] = OMEGA * fl / (4.0 * total + 1.0 - fl)

    def apply(src, x):
        v = src[x]
        gx = FX[x] * (v - src[x - 1]) + FX[x + 1] * (v - src[x + 1])
        gy = FY[x] * (v - up_y(v))
        gz = FZ[x] * (v - up_z(v))
        return FL[x] * (gx + (gy - dn_y(gy)) + (gz - dn_z(gz)))

    def core(v):
        return v[:by, :bz]

    def cycle():
        for x in range(1, ex - 1):
            FIRST[x] = INV[x] * R[x]
        for q in range(1, ex // 2 - 1):
            a, b = 2 * q, 2 * q + 1
            gap = (R[a] - apply(FIRST, a)) + (R[b] - apply(FIRST, b))
            below = IC[q] * pool_yz(gap)
            SEC[a] = FIRST[a] + FL[a] * below
            SEC[b] = FIRST[b] + FL[b] * below
        for x in range(3, ex - 3):
            V[x] = SEC[x] + INV[x] * (R[x] - apply(SEC, x))

    def total(v):
        return jnp.sum(v, axis=(0, 1), keepdims=True)

    width = gath.shape[-1]
    col = lax.broadcasted_iota(jnp.int32, (1, width), 1)

    def spread(row_ref, g, base):
        def send(t, carry):
            remote_row(row_ref, g, base, (me + t) % n).start()
            return carry

        lax.fori_loop(1, n, send, 0)

    def remote_row(row_ref, g, base, flat):
        return pltpu.make_async_remote_copy(
            src_ref=row_ref,
            dst_ref=g.at[me],
            send_sem=send_g.at[base],
            recv_sem=recv_g.at[base],
            device_id=coords(flat),
            device_id_type=MESH,
        )

    def collect(g, base):
        part = g.at[pl.ds(0, n - 1)]
        pltpu.make_async_copy(part, part, recv_g.at[base]).wait()
        pltpu.make_async_copy(part, part, send_g.at[base]).wait()

    cells = bx * by * bz

    cycle()
    sums = [jnp.zeros((by, bz), f32) for _ in range(4)]
    slabs = []
    for x in range(bx):
        e = x + HALO
        av = core(apply(V, e))
        v, r = core(V[e]), core(R[e])
        av_out[x] = av
        tile = edge_tile(av)
        h2_out[x] = tile
        slabs.append((av, tile))
        sums = [sums[0] + r, sums[1] + r * v, sums[2] + v * av, sums[3] + av]
    p2_out[...] = pack(slabs)
    start_all(copies_b)

    acc = jnp.zeros((by, bz), f32)
    for x in range(HALO, HALO + bx):
        acc = acc + core(apply(FL, x))
    faces = []
    for dx, x, near in ((-1, HALO, HALO - 1), (1, HALO + bx, HALO + bx - 1)):
        other = FL[x] if dx == 1 else FL[near]
        mine = FL[near] if dx == 1 else FL[x]
        faces.append(((dx, 0, 0), total(core(FX[x] * mine * other))))
    first_row = wide_row[:by, :bz] == 0
    last_row = wide_row[:by, :bz] == by - 1
    first_lane = wide_lane[:by, :bz] == 0
    last_lane = wide_lane[:by, :bz] == bz - 1
    cy = jnp.zeros((ey, ez), f32)
    cz = jnp.zeros((ey, ez), f32)
    for x in range(HALO, HALO + bx):
        fl = FL[x]
        cy = cy + FY[x] * fl * up_y(fl)
        cz = cz + FZ[x] * fl * up_z(fl)
    cy_hi, cz_hi = core(dn_y(cy)), core(dn_z(cz))
    faces.append(((0, -1, 0), total(jnp.where(first_row, core(cy), 0.0))))
    faces.append(((0, 1, 0), total(jnp.where(last_row, cy_hi, 0.0))))
    faces.append(((0, 0, -1), total(jnp.where(first_lane, core(cz), 0.0))))
    faces.append(((0, 0, 1), total(jnp.where(last_lane, cz_hi, 0.0))))
    diagonal = total(acc)
    row = jnp.zeros((1, width), f32)
    for (dx, dy, dz), g in faces:
        diagonal = diagonal + g
        other = ((ix + dx) * ngy + iy + dy) * ngz + iz + dz
        row = row - jnp.where(col == bz + other, g, 0.0)
    row = row + jnp.where(col == bz + me, diagonal, 0.0)
    for k, part in enumerate(sums):
        row = jnp.where(col == k, total(part), row)
    row_out[...] = row
    gath[pl.ds(me, 1)] = row[None]
    spread(row_out, gath, 0)
    collect(gath, 0)

    def column(g, k):
        return g[:, 0, k : k + 1]

    def solve(means_col):
        y_row = jnp.sum(W * means_col, axis=0, keepdims=True)
        y_col = jnp.sum(jnp.where(eye, y_row, 0.0), axis=1, keepdims=True)
        return y_row, y_col

    ycol_id = lax.broadcasted_iota(jnp.int32, (ey, n), 1)
    yrow_id = lax.broadcasted_iota(jnp.int32, (ey, n), 0)
    dy_id = jnp.where(yrow_id < by, 0, jnp.where(yrow_id < by + HALO, 1, -1))

    def make_table(y_row):
        for dx in (-1, 0, 1):
            cols = []
            for dz in (0, 1, -1):
                where_at = ((ix + dx) * ngy + iy + dy_id) * ngz + iz + dz
                cols.append(
                    jnp.sum(jnp.where(ycol_id == where_at, y_row, 0.0), axis=1, keepdims=True)
                )
            YT[dx + 1] = jnp.concatenate(
                [
                    jnp.broadcast_to(cols[0], (ey, bz)),
                    jnp.where(lane < half, cols[1], cols[2]),
                ],
                axis=1,
            )

    coupling = gath[:, 0, bz : bz + n]
    m0 = column(gath, 0)
    y_row, y_col = solve(m0 * (1.0 / cells))
    rz = total(column(gath, 1)) + total(m0 * y_col)
    dad = (
        total(column(gath, 2))
        + 2.0 * total(column(gath, 3) * y_col)
        + total(coupling * y_col * y_row)
    )
    alpha = rz / dad
    make_table(y_row)
    for x in range(ex):
        U[x] = FL[x] * YT[where_from(x)[0]]

    wait_all(copies_b)
    merged = merge_p(p2_in)
    for x in range(1, ex - 1):
        which, _ = where_from(x)
        au = apply(U, x)
        if which == 1:
            mid = av_out[x - HALO]
        elif which == 0:
            mid = x2_in[0, x]
        else:
            mid = x2_in[1, x - HALO - bx]
        a = jnp.concatenate([mid, merge_h(h2_in, x)], axis=0)
        ad = jnp.concatenate([a, unpack(merged, x, 0)], axis=1) + au
        R[x] = R[x] - alpha * ad
        if which == 1:
            AD0[x - HALO] = core(ad)
            D0[x - HALO] = core(V[x]) + core(U[x])

    cycle()
    sums = [jnp.zeros((by, bz), f32) for _ in range(6)]
    for x in range(bx):
        e = x + HALO
        av = core(apply(V, e))
        v, r, ad0 = core(V[e]), core(R[e]), AD0[x]
        AV1[x] = av
        sums = [
            sums[0] + r,
            sums[1] + r * v,
            sums[2] + v * av,
            sums[3] + av,
            sums[4] + v * ad0,
            sums[5] + ad0,
        ]
    row = jnp.zeros((1, bz), f32)
    for k, part in enumerate(sums):
        row = jnp.where(col[:, :bz] == k, total(part), row)
    row2_out[...] = row
    gath2[pl.ds(me, 1)] = row[None]
    spread(row2_out, gath2, 1)
    collect(gath2, 1)
    m1 = column(gath2, 0)
    y_row, y_col = solve(m1 * (1.0 / cells))
    new = total(column(gath2, 1)) + total(m1 * y_col)
    beta = new / rz
    dad1 = (
        total(column(gath2, 2))
        + 2.0 * total(column(gath2, 3) * y_col)
        + total(coupling * y_col * y_row)
        + 2.0 * beta * (total(column(gath2, 4)) + total(column(gath2, 5) * y_col))
        + beta * beta * dad
    )
    alpha1 = new / dad1
    make_table(y_row)
    for x in range(HALO - 1, HALO + bx + 1):
        U[x] = FL[x] * YT[where_from(x)[0]]
    for x in range(bx):
        e = x + HALO
        d1 = core(V[e]) + core(U[e]) + beta * D0[x]
        ad1 = AV1[x] + core(apply(U, e)) + beta * AD0[x]
        sol_ref[x] = alpha * D0[x] + alpha1 * d1
        res_ref[x] = core(R[e]) - alpha1 * ad1


def solution(mesh):
    counts = (mesh.shape["gx"], mesh.shape["gy"], mesh.shape["gz"])
    n = counts[0] * counts[1] * counts[2]

    def on_device(right_side, conductance, extents, coarse_factor):
        f32 = jnp.float32
        bx, by, bz = right_side.shape
        ex, ey, ez = bx + 2 * HALO, by + 2 * HALO, 2 * bz
        tall = 2 * HALO
        width = bz + -(-n // 128) * 128
        vm = lambda *shape: pltpu.VMEM(shape, f32)
        field = vm(ex, ey, ez)
        dma = pltpu.SemaphoreType.DMA
        scratch = [
            vm(2, bx, tall, bz),
            vm(ey, bz),
            vm(1, bz),
            vm(2, 2, HALO, by, bz),
            vm(2, 2, ex, tall, bz),
            vm(27, ey, bz),
            vm(27, 1, bz),
            vm(bx, by, bz),
            vm(bx, tall, bz),
            vm(ey, bz),
            vm(2, HALO, by, bz),
            vm(2, ex, tall, bz),
            vm(27, ey, bz),
            vm(1, width),
            vm(1, bz),
            vm(n, 1, width),
            vm(n, 1, bz),
            field,
            field,
            field,
            field,
            field,
            field,
            field,
            vm(ex // 2, ey, ez),
            vm(ex // 2, ey, ez),
            field,
            field,
            field,
            field,
            vm(3, ey, ez),
            vm(bx, by, bz),
            vm(bx, by, bz),
            vm(bx, by, bz),
            dma((27, 2)),
            dma((27, 2)),
            dma((27,)),
            dma((27,)),
            dma((27,)),
            dma((27,)),
            dma((2,)),
            dma((2,)),
        ]
        block = jax.ShapeDtypeStruct((bx, by, bz), f32)
        whole = pl.BlockSpec(memory_space=pltpu.VMEM)
        return pl.pallas_call(
            functools.partial(kernel, counts),
            out_shape=(block, block),
            in_specs=[whole, whole, pl.BlockSpec(memory_space=pltpu.SMEM), whole],
            out_specs=(whole, whole),
            scratch_shapes=scratch,
            compiler_params=pltpu.CompilerParams(
                collective_id=0, has_side_effects=True, vmem_limit_bytes=48 * 1024 * 1024
            ),
        )(right_side, conductance, extents, coarse_factor)

    in_specs = (P("gx", "gy", "gz"), P("gx", "gy", "gz"), P("gx", "gy", "gz"), P())
    out_specs = (P("gx", "gy", "gz"), P("gx", "gy", "gz"))
    return jax.shard_map(
        on_device, mesh=mesh, in_specs=in_specs, out_specs=out_specs, check_vma=False
    )
```

time: 366 us -> 33.8 us (0.09)
  blocking collectives: 166 us -> 0 us
  starting transfers between devices: 94.8 us -> 0 us
  waiting for transfers between devices: 36.2 us -> 0 us
  local copies, waits for them, and re-layouts: 34.6 us -> 3.63 us
  Pallas kernels: 0 us -> 28.6 us
  other arithmetic: 21.4 us -> 0 us
  between operations: 7.46 us -> 1.3 us
    psum x3 -> x0, blocking collectives: 126 us -> none  [the longest x2 85.6 us: precondition(): product = lax.psum(local_product, ('gx', 'gy', 'gz'))]
    ppermute x36 -> x0, starting transfers between devices: 94.8 us -> none  [the longest x18 71.6 us: extended(): lax.ppermute(lax.slice_in_dim(block, block.shape[dim] - width, None, axis...]
    unnamed x1 -> x0, blocking collectives: 40.5 us -> none
    ppermute x36 -> x0, waiting for transfers between devices: 36.2 us -> none  [the longest x18 23 us: extended(): lax.ppermute(lax.slice_in_dim(block, 0, width, axis=dim), axis, backward)]
    pallas_call x0 -> x1, Pallas kernels: none -> 28.6 us  [on_device(): pl.pallas_call(functools.partial(kernel, counts), out_shape=(block, block...]
    reshape x5 -> x0, local copies, waits for them, and re-layouts: 25.3 us -> none  [the longest x3 17.3 us: pool_sum(): field.reshape(first // 2, 2, second // 2, 2, third // 2, 2)]
    reduce_sum x7 -> x0, other arithmetic: 10.7 us -> none  [the longest x3 7.64 us: pool_sum(): field.reshape(first // 2, 2, second // 2, 2, third // 2, 2)]
    broadcast_in_dim x2 -> x0, local copies, waits for them, and re-layouts: 5.07 us -> none  [expand(): jnp.broadcast_to(field[:, None, :, None, :, None], (first, 2, second, 2,...]
  transfers between devices with their start and end apart: 36 -> 0, of which waited for: 16 -> 0; matrix products, arithmetic and copies ran while one was open for 7% -> 0% of each run, Pallas kernels for 0% -> 0%
where the time goes in v1:
time: 33.8 us; the launch traced here: 33.5 us
  Pallas kernels  28.6 us (85%)
  local copies, waits for them, and re-layouts  3.63 us (11%)
  between operations  1.3 us (4%)
    pallas_call x1, Pallas kernels, on_device(): pl.pallas_call(functools.partial(kernel, counts), out_shape=(block, block...  28.6 us
    unnamed x8, local copies, waits for them, and re-layouts  3.63 us

profile of v1, /device:TPU:0, one launch (start us, length us, event | category | flops | bytes accessed | tf_op | source)
XLA Modules:
  0.0 33.5 jit_solution(5004659747924598773)
XLA Ops:
  1.3 0.0 copy-start
  1.3 0.8 %copy-done = f32[8,16,128]{2,1,0:T(8,128)S(1)} copy-done((f32[8,16,128]{2,1,0:T(8,128)S(1)}, f32[8,16,128]{2,1,0:T(8,128)}, u32[]{:S(2)}) %copy-start) | copy-done | bytes 65560
  2.1 0.0 copy-start.1
  2.1 0.8 %copy-done.1 = f32[8,16,128]{2,1,0:T(8,128)S(1)} copy-done((f32[8,16,128]{2,1,0:T(8,128)S(1)}, f32[8,16,128]{2,1,0:T(8,128)}, u32[]{:S(2)}) %copy-start.1) | copy-done | bytes 65560
  3.0 0.0 copy-start.2
  3.0 0.7 %copy-done.2 = bf16[32,32]{1,0:T(8,128)(2,1)S(1)} copy-done((bf16[32,32]{1,0:T(8,128)(2,1)S(1)}, bf16[32,32]{1,0:T(8,128)(2,1)}, u32[]{:S(2)}) %copy-start.2) | copy-done | bytes 2072
  3.7 28.6 %shard_map.59 = (f32[8,16,128]{2,1,0:T(8,128)S(1)}, f32[8,16,128]{2,1,0:T(8,128)S(1)}) custom-call(f32[8,16,128]{2,1,0:T(8,128)S(1)} %copy-done, f32[8,16,128]{2,1,0:T(8,128)S(1)} %copy-done.1, s32[1,1,1]{2,1,0:T(1,128)S(6)} %copy.8.ext_ref, bf16[32,32]{1,0:T(8,128)(2,1)S(1)} %copy-done.2), custom_call_target="tpu_custom_call" | custom-call | tf_op jit(solution)/shard_map/pallas_call | solution.py:640
  32.3 0.6 %copy.9 = f32[8,16,128]{2,1,0:T(8,128)} copy(f32[8,16,128]{2,1,0:T(8,128)S(1)} %get-tuple-element.4) | data formatting | bytes 131072
  32.9 0.6 %copy.10 = f32[8,16,128]{2,1,0:T(8,128)} copy(f32[8,16,128]{2,1,0:T(8,128)S(1)} %get-tuple-element.5) | data formatting | bytes 131072
Async XLA Ops:
  1.3 0.8 %copy-start = (f32[8,16,128]{2,1,0:T(8,128)S(1)}, f32[8,16,128]{2,1,0:T(8,128)}, u32[]{:S(2)}) copy-start(f32[8,16,128]{2,1,0:T(8,128)} %rhs_ref.1) | copy-start | bytes 196612
  2.1 0.8 %copy-start.1 = (f32[8,16,128]{2,1,0:T(8,128)S(1)}, f32[8,16,128]{2,1,0:T(8,128)}, u32[]{:S(2)}) copy-start(f32[8,16,128]{2,1,0:T(8,128)} %cond_ref.1) | copy-start | bytes 196612
  3.0 0.7 %copy-start.2 = (bf16[32,32]{1,0:T(8,128)(2,1)S(1)}, bf16[32,32]{1,0:T(8,128)(2,1)}, u32[]{:S(2)}) copy-start(bf16[32,32]{1,0:T(8,128)(2,1)} %factor_ref.1) | copy-start | bytes 6148

commit v2 on v1

--- a/solution.py
+++ b/solution.py
@@ -18,6 +18,7 @@
     for dz in (-1, 0, 1)
     if (dx, dy, dz) != (0, 0, 0)
 ]
+DIRS.sort(key=lambda d: -sum(abs(a) for a in d))
 
 
 def code(dx, dy, dz):
@@ -26,12 +27,15 @@
 
 def kernel(
     counts,
+    rhs_hbm,
+    cond_hbm,
+    ext_ref,
+    factor_hbm,
+    sol_ref,
+    res_ref,
     rhs_ref,
     cond_ref,
-    ext_ref,
     factor_ref,
-    sol_ref,
-    res_ref,
     h_out,
     p_out,
     e_out,
@@ -74,6 +78,7 @@
     recv_b,
     send_g,
     recv_g,
+    load_sem,
 ):
     ngx, ngy, ngz = counts
     n = ngx * ngy * ngz
@@ -85,26 +90,63 @@
     half = bz // 2
     f32 = jnp.float32
 
-    def coords(flat):
-        return (flat // (ngy * ngz), (flat // ngz) % ngy, flat % ngz)
-
-    barrier = pltpu.get_barrier_semaphore()
-
-    def greet(t, carry):
-        pl.semaphore_signal(
-            barrier, inc=1, device_id=coords((me + t) % n), device_id_type=MESH
-        )
-        return carry
+    loads = [
+        pltpu.make_async_copy(src, dst, load_sem.at[k])
+        for k, (src, dst) in enumerate(
+            ((rhs_hbm, rhs_ref), (cond_hbm, cond_ref), (factor_hbm, factor_ref))
+        )
+    ]
+    for load in loads:
+        load.start()
+
+    def turned(at, step, count):
+        moved = at + step
+        return jnp.where(moved >= count, moved - count, moved)
+
+    def everyone(act):
+        if n <= 64:
+            xs = [turned(ix, t, ngx) for t in range(ngx)]
+            ys = [turned(iy, t, ngy) for t in range(ngy)]
+            zs = [turned(iz, t, ngz) for t in range(ngz)]
+            steps = [(a, b, c) for a in range(ngx) for b in range(ngy) for c in range(ngz)]
+            steps.sort(
+                key=lambda t: -sum(min(a, m - a) for a, m in zip(t, (ngx, ngy, ngz)))
+            )
+            for a, b, c in steps[:-1]:
+                act((xs[a], ys[b], zs[c]))
+        else:
+
+            def one(t, carry):
+                flat = (me + t) % n
+                act((flat // (ngy * ngz), (flat // ngz) % ngy, flat % ngz))
+                return carry
+
+            lax.fori_loop(1, n, one, 0)
 
     for buf in (x_in, h_in, p_in, e_in, x2_in, h2_in, p2_in):
         buf[...] = jnp.zeros(buf.shape, f32)
-    lax.fori_loop(1, n, greet, 0)
+
+    barrier = pltpu.get_barrier_semaphore()
+    everyone(
+        lambda device: pl.semaphore_signal(
+            barrier, inc=1, device_id=device, device_id_type=MESH
+        )
+    )
 
     lane = lax.broadcasted_iota(jnp.int32, (ey, bz), 1)
     row8 = lax.broadcasted_iota(jnp.int32, (2 * HALO, bz), 0)
 
     def edge_tile(slab):
         return jnp.where(row8 < HALO, slab[: 2 * HALO], slab[by - 2 * HALO :])
+
+    def pack_pairs(out, lows, highs):
+        for p in range(len(lows) // 2):
+            out[0][p] = jnp.where(
+                row8 < HALO, pltpu.roll(highs[2 * p], HALO, 0), highs[2 * p + 1]
+            )
+            out[1][p] = jnp.where(
+                row8 < HALO, lows[2 * p], pltpu.roll(lows[2 * p + 1], HALO, 0)
+            )
 
     def pack(slabs):
         packed = jnp.zeros((ey, bz), f32)
@@ -114,17 +156,146 @@
             packed = jnp.where(lane // group == at, moved, packed)
         return packed
 
+    for load in loads[:2]:
+        load.wait()
+    tall = 2 * HALO
     slabs = []
     for f, ref in enumerate((rhs_ref, cond_ref)):
-        for x in range(bx):
-            slab = ref[x]
-            tile = edge_tile(slab)
-            h_out[f, x] = tile
-            slabs.append((slab, tile))
+        fields = [ref[x] for x in range(bx)]
+        pack_pairs(
+            (h_out.at[0, f], h_out.at[1, f]),
+            [v[:tall] for v in fields],
+            [v[by - tall :] for v in fields],
+        )
+        slabs.extend((v, edge_tile(v)) for v in fields)
     p_out[...] = pack(slabs)
     own_limit = ext_ref[0, 0, 0]
     e_out[...] = jnp.full((1, bz), own_limit.astype(f32), f32)
 
+    pl.semaphore_wait(barrier, n - 1)
+
+    def inside(d):
+        dx, dy, dz = d
+        ok = None
+        for at, step, count in ((ix, dx, ngx), (iy, dy, ngy), (iz, dz, ngz)):
+            if step == 0:
+                continue
+            here = (at + step >= 0) & (at + step < count)
+            ok = here if ok is None else ok & here
+        return ok
+
+    def target(d):
+        return (ix + d[0], iy + d[1], iz + d[2])
+
+    def remote(src, dst, send, recv, d):
+        return pltpu.make_async_remote_copy(
+            src_ref=src,
+            dst_ref=dst,
+            send_sem=send,
+            recv_sem=recv,
+            device_id=target(d),
+            device_id_type=MESH,
+        )
+
+    def x_part(dx):
+        return pl.ds(bx - HALO, HALO) if dx == 1 else pl.ds(0, HALO)
+
+    def pair_part(dx):
+        few, all_ = HALO // 2, bx // 2
+        if dx == 0:
+            return pl.ds(0, all_), pl.ds(few, all_)
+        if dx == 1:
+            return pl.ds(all_ - few, few), pl.ds(0, few)
+        return pl.ds(0, few), pl.ds(all_ + few, few)
+
+    def p_rows(dy):
+        return pl.ds(0, by) if dy == 0 else pl.ds(by, tall)
+
+    def side(dx):
+        return 0 if dx == 1 else 1
+
+    def copies_a(d):
+        dx, dy, dz = d
+        k = code(*d)
+        out = [remote(e_out, e_in.at[code(-dx, -dy, -dz)], send_e.at[k], recv_e.at[k], d)]
+        if dz != 0:
+            slot = code(-dx, -dy, -dz)
+            rows = p_rows(dy)
+            out.append(
+                remote(
+                    p_out.at[rows], p_in.at[slot, rows], send_a.at[k, 0], recv_a.at[k, 0], d
+                )
+            )
+        elif dy != 0:
+            src, dst = pair_part(dx)
+            out.append(
+                remote(
+                    h_out.at[side(dy), :, src],
+                    h_in.at[side(dy), :, dst],
+                    send_a.at[k, 0],
+                    recv_a.at[k, 0],
+                    d,
+                )
+            )
+        else:
+            src = x_part(dx)
+            for f, ref in enumerate((rhs_ref, cond_ref)):
+                out.append(
+                    remote(
+                        ref.at[src],
+                        x_in.at[side(dx), f],
+                        send_a.at[k, f],
+                        recv_a.at[k, f],
+                        d,
+                    )
+                )
+        return out
+
+    def copies_b(d):
+        dx, dy, dz = d
+        k = code(*d)
+        if dz != 0:
+            slot = code(-dx, -dy, -dz)
+            rows = p_rows(dy)
+            return [
+                remote(p2_out.at[rows], p2_in.at[slot, rows], send_b.at[k], recv_b.at[k], d)
+            ]
+        if dy != 0:
+            src, dst = pair_part(dx)
+            return [
+                remote(
+                    h2_out.at[side(dy), src], h2_in.at[side(dy), dst], send_b.at[k], recv_b.at[k], d
+                )
+            ]
+        src = x_part(dx)
+        return [remote(av_out.at[src], x2_in.at[side(dx)], send_b.at[k], recv_b.at[k], d)]
+
+    def start_all(copies):
+        for d in DIRS:
+
+            @pl.when(inside(d))
+            def _():
+                for c in copies(d):
+                    c.start()
+
+    def wait_all(copies):
+        for d in DIRS:
+            @pl.when(inside(tuple(-a for a in d)))
+            def _():
+                for c in copies(d):
+                    c.wait_recv()
+
+    def wait_sent(copies):
+        for d in DIRS:
+
+            @pl.when(inside(d))
+            def _():
+                for c in copies(d):
+                    c.wait_send()
+
+    start_all(copies_a)
+
+    loads[2].wait()
     L = factor_ref[...].astype(f32)
     ri = lax.broadcasted_iota(jnp.int32, (n, n), 0)
     ci = lax.broadcasted_iota(jnp.int32, (n, n), 1)
@@ -145,117 +316,14 @@
         X, X, (((0,), (0,)), ((), ())), precision=HIGH, preferred_element_type=f32
     )
 
-    pl.semaphore_wait(barrier, n - 1)
-
-    def inside(d):
-        dx, dy, dz = d
-        ok = None
-        for at, step, count in ((ix, dx, ngx), (iy, dy, ngy), (iz, dz, ngz)):
-            if step == 0:
-                continue
-            here = (at + step >= 0) & (at + step < count)
-            ok = here if ok is None else ok & here
-        return ok
-
-    def target(d):
-        return (ix + d[0], iy + d[1], iz + d[2])
-
-    def remote(src, dst, send, recv, d):
-        return pltpu.make_async_remote_copy(
-            src_ref=src,
-            dst_ref=dst,
-            send_sem=send,
-            recv_sem=recv,
-            device_id=target(d),
-            device_id_type=MESH,
-        )
-
-    def x_part(dx):
-        if dx == 0:
-            return pl.ds(0, bx), pl.ds(HALO, bx)
-        if dx == 1:
-            return pl.ds(bx - HALO, HALO), pl.ds(0, HALO)
-        return pl.ds(0, HALO), pl.ds(bx + HALO, HALO)
-
-    def side(dx):
-        return 0 if dx == 1 else 1
-
-    def copies_a(d):
-        dx, dy, dz = d
-        k = code(*d)
-        out = [remote(e_out, e_in.at[code(-dx, -dy, -dz)], send_e.at[k], recv_e.at[k], d)]
-        if dz != 0:
-            slot = code(-dx, -dy, -dz)
-            out.append(remote(p_out, p_in.at[slot], send_a.at[k, 0], recv_a.at[k, 0], d))
-        elif dy != 0:
-            src, dst = x_part(dx)
-            out.append(
-                remote(
-                    h_out.at[:, src],
-                    h_in.at[side(dy), :, dst],
-                    send_a.at[k, 0],
-                    recv_a.at[k, 0],
-                    d,
-                )
-            )
-        else:
-            src, _ = x_part(dx)
-            for f, ref in enumerate((rhs_ref, cond_ref)):
-                out.append(
-                    remote(
-                        ref.at[src],
-                        x_in.at[side(dx), f],
-                        send_a.at[k, f],
-                        recv_a.at[k, f],
-                        d,
-                    )
-                )
-        return out
-
-    def copies_b(d):
-        dx, dy, dz = d
-        k = code(*d)
-        if dz != 0:
-            slot = code(-dx, -dy, -dz)
-            return [remote(p2_out, p2_in.at[slot], send_b.at[k], recv_b.at[k], d)]
-        src, dst = x_part(dx)
-        if dy != 0:
-            return [
-                remote(
-                    h2_out.at[src], h2_in.at[side(dy), dst], send_b.at[k], recv_b.at[k], d
-                )
-            ]
-        return [remote(av_out.at[src], x2_in.at[side(dx)], send_b.at[k], recv_b.at[k], d)]
-
-    def start_all(copies):
-        for d in DIRS:
-
-            @pl.when(inside(d))
-            def _():
-                for c in copies(d):
-                    c.start()
-
-    def wait_all(copies):
-        for d in DIRS:
-            @pl.when(inside(tuple(-a for a in d)))
-            def _():
-                for c in copies(d):
-                    c.wait_recv()
-
-        for d in DIRS:
-
-            @pl.when(inside(d))
-            def _():
-                for c in copies(d):
-                    c.wait_send()
-
-    start_all(copies_a)
-
     rowe = lax.broadcasted_iota(jnp.int32, (ey, bz), 0)
     low_lanes = (lane % group) < HALO
 
-    def merge_h(h, *at):
-        return jnp.where(row8 < HALO, h[(1,) + at], h[(0,) + at])
+    def merge_h(h, x, *at):
+        low, high = h[(0,) + at + (x // 2,)], h[(1,) + at + (x // 2,)]
+        if x % 2 == 0:
+            return jnp.where(row8 < HALO, high, pltpu.roll(low, HALO, 0))
+        return jnp.where(row8 < HALO, pltpu.roll(high, HALO, 0), low)
 
     def merge_p(p):
         merged = []
@@ -323,7 +391,7 @@
                 core = x_in[0, f, x]
             else:
                 core = x_in[1, f, x - HALO - bx]
-            a = jnp.concatenate([core, merge_h(h_in, f, x)], axis=0)
+            a = jnp.concatenate([core, merge_h(h_in, x, f)], axis=0)
             whole = jnp.concatenate([a, unpack(merged, x, f)], axis=1)
             field[x] = whole * flags[which] if f == 0 else whole
 
@@ -398,19 +466,15 @@
     col = lax.broadcasted_iota(jnp.int32, (1, width), 1)
 
     def spread(row_ref, g, base):
-        def send(t, carry):
-            remote_row(row_ref, g, base, (me + t) % n).start()
-            return carry
-
-        lax.fori_loop(1, n, send, 0)
-
-    def remote_row(row_ref, g, base, flat):
+        everyone(lambda device: remote_row(row_ref, g, base, device).start())
+
+    def remote_row(row_ref, g, base, device):
         return pltpu.make_async_remote_copy(
             src_ref=row_ref,
             dst_ref=g.at[me],
             send_sem=send_g.at[base],
             recv_sem=recv_g.at[base],
-            device_id=coords(flat),
+            device_id=device,
             device_id_type=MESH,
         )
 
@@ -429,10 +493,13 @@
         av = core(apply(V, e))
         v, r = core(V[e]), core(R[e])
         av_out[x] = av
-        tile = edge_tile(av)
-        h2_out[x] = tile
-        slabs.append((av, tile))
+        slabs.append((av, edge_tile(av)))
         sums = [sums[0] + r, sums[1] + r * v, sums[2] + v * av, sums[3] + av]
+    pack_pairs(
+        (h2_out.at[0], h2_out.at[1]),
+        [v[:tall] for v, _ in slabs],
+        [v[by - tall :] for v, _ in slabs],
+    )
     p2_out[...] = pack(slabs)
     start_all(copies_b)
 
@@ -576,6 +643,8 @@
         ad1 = AV1[x] + core(apply(U, e)) + beta * AD0[x]
         sol_ref[x] = alpha * D0[x] + alpha1 * d1
         res_ref[x] = core(R[e]) - alpha1 * ad1
+    wait_sent(copies_a)
+    wait_sent(copies_b)
 
 
 def solution(mesh):
@@ -592,18 +661,21 @@
         field = vm(ex, ey, ez)
         dma = pltpu.SemaphoreType.DMA
         scratch = [
-            vm(2, bx, tall, bz),
+            vm(bx, by, bz),
+            vm(bx, by, bz),
+            pltpu.VMEM(coarse_factor.shape, coarse_factor.dtype),
+            vm(2, 2, bx // 2, tall, bz),
             vm(ey, bz),
             vm(1, bz),
             vm(2, 2, HALO, by, bz),
-            vm(2, 2, ex, tall, bz),
+            vm(2, 2, ex // 2, tall, bz),
             vm(27, ey, bz),
             vm(27, 1, bz),
             vm(bx, by, bz),
-            vm(bx, tall, bz),
+            vm(2, bx // 2, tall, bz),
             vm(ey, bz),
             vm(2, HALO, by, bz),
-            vm(2, ex, tall, bz),
+            vm(2, ex // 2, tall, bz),
             vm(27, ey, bz),
             vm(1, width),
             vm(1, bz),
@@ -634,17 +706,19 @@
             dma((27,)),
             dma((2,)),
             dma((2,)),
+            dma((3,)),
         ]
         block = jax.ShapeDtypeStruct((bx, by, bz), f32)
         whole = pl.BlockSpec(memory_space=pltpu.VMEM)
+        outer = pl.BlockSpec(memory_space=pltpu.HBM)
         return pl.pallas_call(
             functools.partial(kernel, counts),
             out_shape=(block, block),
-            in_specs=[whole, whole, pl.BlockSpec(memory_space=pltpu.SMEM), whole],
+            in_specs=[outer, outer, pl.BlockSpec(memory_space=pltpu.SMEM), outer],
             out_specs=(whole, whole),
             scratch_shapes=scratch,
             compiler_params=pltpu.CompilerParams(
-                collective_id=0, has_side_effects=True, vmem_limit_bytes=48 * 1024 * 1024
+                collective_id=0, has_side_effects=True, vmem_limit_bytes=67043328
             ),
         )(right_side, conductance, extents, coarse_factor)
 

time: 33.8 us -> 29.2 us (0.86)
  Pallas kernels: 28.6 us -> 25.5 us
  local copies, waits for them, and re-layouts: 3.63 us -> 2.14 us
    pallas_call x1, Pallas kernels: 28.6 us -> 25.5 us  [on_device(): pl.pallas_call(functools.partial(kernel, counts), out_shape=(block, block...]
    unnamed x8 -> x4, local copies, waits for them, and re-layouts: 3.63 us -> 2.14 us
where the time goes in v2:
time: 29.2 us; the launch traced here: 29 us
  Pallas kernels  25.5 us (87%)
  local copies, waits for them, and re-layouts  2.14 us (7%)
  between operations  1.29 us (4%)
    pallas_call x1, Pallas kernels, on_device(): pl.pallas_call(functools.partial(kernel, counts), out_shape=(block, block...  25.5 us
    unnamed x4, local copies, waits for them, and re-layouts  2.14 us

profile of v2, /device:TPU:0, one launch (start us, length us, event | category | flops | bytes accessed | tf_op | source)
XLA Modules:
  0.0 29.0 jit_solution(2445907258195368791)
XLA Ops:
  1.3 25.5 %shard_map.59 = (f32[8,16,128]{2,1,0:T(8,128)}, f32[8,16,128]{2,1,0:T(8,128)}) custom-call(f32[8,16,128]{2,1,0:T(8,128)} %rhs_hbm.1, f32[8,16,128]{2,1,0:T(8,128)} %cond_hbm.1, s32[1,1,1]{2,1,0:T(1,128)S(6)} %copy.8.ext_ref, bf16[32,32]{1,0:T(8,128)(2,1)} %factor_hbm.1), custom_call_target="tpu_custom_call" | custom-call | tf_op jit(solution)/shard_map/pallas_call | solution.py:714
  26.8 0.0 copy-start
  26.8 1.5 %copy.9 = f32[8,16,128]{2,1,0:T(8,128)} copy(f32[8,16,128]{2,1,0:T(8,128)} %get-tuple-element.4) | data formatting | bytes 131072
  28.3 0.0 copy-done
  28.3 0.6 %copy.10 = f32[8,16,128]{2,1,0:T(8,128)} copy(f32[8,16,128]{2,1,0:T(8,128)S(1)} %copy-done) | data formatting | bytes 131072
Async XLA Ops:
  26.8 1.5 %copy-start = (f32[8,16,128]{2,1,0:T(8,128)S(1)}, f32[8,16,128]{2,1,0:T(8,128)}, u32[]{:S(2)}) copy-start(f32[8,16,128]{2,1,0:T(8,128)} %get-tuple-element.5) | copy-start | bytes 196612

commit v3 on v2

--- a/solution.py
+++ b/solution.py
@@ -708,7 +708,7 @@
             dma((2,)),
             dma((3,)),
         ]
-        block = jax.ShapeDtypeStruct((bx, by, bz), f32)
+        block = vm(bx, by, bz)
         whole = pl.BlockSpec(memory_space=pltpu.VMEM)
         outer = pl.BlockSpec(memory_space=pltpu.HBM)
         return pl.pallas_call(
@@ -718,7 +718,7 @@
             out_specs=(whole, whole),
             scratch_shapes=scratch,
             compiler_params=pltpu.CompilerParams(
-                collective_id=0, has_side_effects=True, vmem_limit_bytes=67043328
+                collective_id=0, has_side_effects=True, vmem_limit_bytes=60000000
             ),
         )(right_side, conductance, extents, coarse_factor)
 

time: 29.2 us -> 27.6 us (0.945)
  local copies, waits for them, and re-layouts: 2.14 us -> 1.26 us
  Pallas kernels: 25.5 us -> 24.9 us
    unnamed x4 -> x2, local copies, waits for them, and re-layouts: 2.14 us -> 1.26 us
    pallas_call x1, Pallas kernels: 25.5 us -> 24.9 us  [on_device(): pl.pallas_call(functools.partial(kernel, counts), out_shape=(block, block...]
where the time goes in v3:
time: 27.6 us; the launch traced here: 27.4 us
  Pallas kernels  24.9 us (90%)
  between operations  1.28 us (5%)
  local copies, waits for them, and re-layouts  1.26 us (5%)
    pallas_call x1, Pallas kernels, on_device(): pl.pallas_call(functools.partial(kernel, counts), out_shape=(block, block...  24.9 us
    unnamed x2, local copies, waits for them, and re-layouts  1.26 us

profile of v3, /device:TPU:0, one launch (start us, length us, event | category | flops | bytes accessed | tf_op | source)
XLA Modules:
  0.0 27.4 jit_solution(9182481158106327158)
XLA Ops:
  1.3 24.9 %shard_map.59 = (f32[8,16,128]{2,1,0:T(8,128)S(1)}, f32[8,16,128]{2,1,0:T(8,128)S(1)}) custom-call(f32[8,16,128]{2,1,0:T(8,128)} %rhs_hbm.1, f32[8,16,128]{2,1,0:T(8,128)} %cond_hbm.1, s32[1,1,1]{2,1,0:T(1,128)S(6)} %copy.10.ext_ref, bf16[32,32]{1,0:T(8,128)(2,1)} %factor_hbm.1), custom_call_target="tpu_custom_call" | custom-call | tf_op jit(solution)/shard_map/pallas_call | solution.py:714
  26.2 0.6 %copy.8 = f32[8,16,128]{2,1,0:T(8,128)} copy(f32[8,16,128]{2,1,0:T(8,128)S(1)} %get-tuple-element.2) | data formatting | bytes 131072
  26.8 0.6 %copy.9 = f32[8,16,128]{2,1,0:T(8,128)} copy(f32[8,16,128]{2,1,0:T(8,128)S(1)} %get-tuple-element.3) | data formatting | bytes 131072
